TPU v7x, 32 devices: a whole 2x2x4 slice. The times are simulated.
32 devices in a mesh: dp: 16 (over z, y, core), tensor: 2 (over x).
Axes of the slice: x: 2, y: 2, z: 4, core: 2. Of those that a mesh axis runs over, the one named last changes fastest.
Arguments:
- tokens: bfloat16 [21760, 1024], P('dp'), may hold values from -6 to 6
- d_out: bfloat16 [21760, 1024], P('dp'), may hold values from -6 to 6
- labels: int32 [32], replicated, may hold values from 0 to 999
- scale_ids: int32 [32, 680], P('dp'), may hold values from 0 to 9, never falling along the last dimension, each value on 1 to 256 neighbouring positions
- class_table: bfloat16 [1000, 1024], P(None, 'tensor'), may hold values from -6 to 6
- ada_weight: bfloat16 [1024, 6144], P(None, 'tensor'), may hold values from -0.1875 to 0.1875
- ada_bias: bfloat16 [6144], P('tensor'), may hold values from -3 to 3
- qkv_weight: bfloat16 [1024, 3, 1024], P(None, None, 'tensor'), may hold values from -0.1875 to 0.1875
- q_bias: bfloat16 [1024], P('tensor'), may hold values from -3 to 3
- v_bias: bfloat16 [1024], P('tensor'), may hold values from -3 to 3
- qk_scale: float32 [16], P('tensor'), may hold values from 2.3 to 3
- proj_weight: bfloat16 [1024, 1024], P('tensor'), may hold values from -0.75 to 0.75
- proj_bias: bfloat16 [1024], replicated, may hold values from -2 to 2
- fc1_weight: bfloat16 [1024, 4096], P(None, 'tensor'), may hold values from -0.1875 to 0.1875
- fc1_bias: bfloat16 [4096], P('tensor'), may hold values from -2 to 2
- fc2_weight: bfloat16 [4096, 1024], P('tensor'), may hold values from -0.1875 to 0.1875
- fc2_bias: bfloat16 [1024], replicated, may hold values from -2 to 2
Outputs:
- out: bfloat16 [21760, 1024], P('dp')
- d_tokens: bfloat16 [21760, 1024], P('dp')
- grad_table: float32 [1000, 1024], P(None, 'tensor')
- grad_ada: float32 [1024, 6144], P(None, 'tensor')
- grad_ada_bias: float32 [6144], P('tensor')
- grad_qkv: float32 [1024, 3, 1024], P(None, None, 'tensor')
- grad_q_bias: float32 [1024], P('tensor')
- grad_v_bias: float32 [1024], P('tensor')
- grad_qk_scale: float32 [16], P('tensor')
- grad_proj: float32 [1024, 1024], P('tensor')
- grad_proj_bias: float32 [1024], replicated
- grad_fc1: float32 [1024, 4096], P(None, 'tensor')
- grad_fc1_bias: float32 [4096], P('tensor')
- grad_fc2: float32 [4096, 1024], P('tensor')
- grad_fc2_bias: float32 [1024], replicated
Inputs may be any that keep to these rules, and one draw needn't show every extreme that they name: `scale_ids`: in each image the scale indices never fall, each of the 10 scales holds 1 to 256 tokens, and some scale of every image holds exactly 256.
All inputs are finite; a program needn't handle non-finite values.
Results may differ from a plain program's by a relative error of at most 0.033.
Values may be sent and summed in bfloat16 or wider, within the bound.
A program may use at most 320 MiB of HBM per device.

v0:
```python
from functools import partial
import jax
import jax.numpy as jnp
from jax import lax
from jax.sharding import PartitionSpec as P

epsilon = 1e-06
highest = lax.Precision.HIGHEST


def tensor_sum(part):
    if lax.axis_size("tensor") == 2:
        other = lax.ppermute(part, "tensor", [(0, 1), (1, 0)])
        return part.astype(jnp.float32) + other.astype(jnp.float32)
    return lax.psum(part, "tensor").astype(jnp.float32)


def layer_stats(values):
    center = values - jnp.mean(values, axis=-1, keepdims=True)
    inv_std = lax.rsqrt(jnp.mean(center * center, axis=-1, keepdims=True) + epsilon)
    return (center * inv_std, inv_std)


def layer_back(d_normed, normed, inv_std):
    first_mean = jnp.mean(d_normed, axis=-1, keepdims=True)
    second_mean = jnp.mean(d_normed * normed, axis=-1, keepdims=True)
    return inv_std * (d_normed - first_mean - normed * second_mean)


def per_device(
    tokens,
    d_out,
    labels,
    scale_ids,
    class_table,
    ada_weight,
    ada_bias,
    qkv_weight,
    q_bias,
    v_bias,
    qk_scale,
    proj_weight,
    proj_bias,
    fc1_weight,
    fc1_bias,
    fc2_weight,
    fc2_bias,
):
    f32 = jnp.float32
    bf16 = jnp.bfloat16
    images = scale_ids.shape[0]
    length = scale_ids.shape[1]
    model_width = tokens.shape[1]
    rows_all = images * length
    classes = class_table.shape[0]
    heads_here = qk_scale.shape[0]
    local_width = qkv_weight.shape[2]
    head_size = local_width // heads_here
    mod_width = ada_weight.shape[1]
    first_image = lax.axis_index("dp") * images
    class_ids = jnp.arange(classes, dtype=jnp.int32)
    pick_all = labels[:, None] == class_ids[None, :]
    cond_all_cols = jnp.dot(pick_all.astype(bf16), class_table, preferred_element_type=f32)
    cond_all = lax.all_gather(cond_all_cols.astype(bf16), "tensor", axis=1, tiled=True)
    cond_full = lax.dynamic_slice_in_dim(cond_all, first_image, images)
    act_cond = jax.nn.silu(cond_full.astype(f32)).astype(bf16)
    mod_cols = jnp.dot(act_cond, ada_weight, preferred_element_type=f32) + ada_bias.astype(f32)
    modul = lax.all_gather(mod_cols, "tensor", axis=1, tiled=True)
    gain_one, gain_two, scale_one, scale_two, shift_one, shift_two = [
        modul[:, None, member * model_width : (member + 1) * model_width] for member in range(6)
    ]
    inputs = tokens.astype(f32).reshape(images, length, model_width)
    normed_one, inv_std_one = layer_stats(inputs)
    hidden_one = (
        (normed_one * (1.0 + scale_one) + shift_one).astype(bf16).reshape(rows_all, model_width)
    )
    bias_stack = jnp.stack([q_bias.astype(f32), jnp.zeros(q_bias.shape, f32), v_bias.astype(f32)])
    qkv_val = (
        jnp.einsum("rd,dpc->rpc", hidden_one, qkv_weight, preferred_element_type=f32)
        + bias_stack[None]
    )
    qkv_val = qkv_val.reshape(images, length, 3, heads_here, head_size)
    query_raw = qkv_val[:, :, 0]
    key_raw = qkv_val[:, :, 1]
    value_raw = qkv_val[:, :, 2]
    query_inv = lax.rsqrt(jnp.sum(query_raw * query_raw, axis=-1, keepdims=True) + epsilon)
    query_unit = query_raw * query_inv
    growth = jnp.exp(qk_scale)[None, None, :, None]
    query_scaled = query_unit * growth
    query_low = query_scaled.astype(bf16)
    key_inv = lax.rsqrt(jnp.sum(key_raw * key_raw, axis=-1, keepdims=True) + epsilon)
    key_unit = key_raw * key_inv
    key_low = key_unit.astype(bf16)
    value_low = value_raw.astype(bf16)
    allowed = scale_ids[:, None, None, :] <= scale_ids[:, None, :, None]

    def masked_scores():
        scores = jnp.einsum("ishe,ithe->ihst", query_low, key_low, preferred_element_type=f32)
        return jnp.where(allowed, scores, f32(-1e30))

    masked = masked_scores()
    row_max = jnp.max(masked, axis=-1, keepdims=True)
    weights_exp = jnp.exp(masked - row_max)
    row_total = jnp.sum(weights_exp, axis=-1, keepdims=True)
    log_total = row_max + jnp.log(row_total)
    probs_low = (weights_exp / row_total).astype(bf16)
    attn_out = (
        jnp.einsum("ihst,ithe->ishe", probs_low, value_low, preferred_element_type=f32)
        .reshape(rows_all, local_width)
        .astype(bf16)
    )
    gelu_tanh = partial(jax.nn.gelu, approximate=True)
    d_result = d_out.astype(f32).reshape(images, length, model_width)
    branch_one = tensor_sum(jnp.dot(attn_out, proj_weight, preferred_element_type=f32).astype(bf16))
    branch_one = (branch_one + proj_bias.astype(f32)).reshape(images, length, model_width)
    middle = inputs + gain_one * branch_one
    normed_two, inv_std_two = layer_stats(middle)
    hidden_two = (
        (normed_two * (1.0 + scale_two) + shift_two).astype(bf16).reshape(rows_all, model_width)
    )
    pre_act = jnp.dot(hidden_two, fc1_weight, preferred_element_type=f32) + fc1_bias.astype(f32)
    mlp_low = gelu_tanh(pre_act).astype(bf16)
    branch_two = tensor_sum(jnp.dot(mlp_low, fc2_weight, preferred_element_type=f32).astype(bf16))
    branch_two = (branch_two + fc2_bias.astype(f32)).reshape(images, length, model_width)
    result = (middle + gain_two * branch_two).astype(bf16).reshape(rows_all, model_width)
    d_branch_two = (gain_two * d_result).astype(bf16).reshape(rows_all, model_width)
    grad_fc2 = jnp.einsum("rf,rd->fd", mlp_low, d_branch_two, preferred_element_type=f32)
    grad_fc2_bias = jnp.sum(d_branch_two.astype(f32), axis=0)
    d_mlp = jnp.einsum("rd,fd->rf", d_branch_two, fc2_weight, preferred_element_type=f32)
    gelu_value, gelu_pull = jax.vjp(gelu_tanh, pre_act)
    d_pre = gelu_pull(d_mlp)[0].astype(bf16)
    grad_fc1 = jnp.einsum("rd,rf->df", hidden_two, d_pre, preferred_element_type=f32)
    grad_fc1_bias = jnp.sum(d_pre.astype(f32), axis=0)
    d_hidden_two = tensor_sum(
        jnp.einsum("rf,df->rd", d_pre, fc1_weight, preferred_element_type=f32).astype(bf16)
    )
    d_hidden_two = d_hidden_two.reshape(images, length, model_width)
    d_middle = d_result + layer_back(d_hidden_two * (1.0 + scale_two), normed_two, inv_std_two)
    d_branch_one = (gain_one * d_middle).astype(bf16).reshape(rows_all, model_width)
    grad_proj = jnp.einsum("rc,rd->cd", attn_out, d_branch_one, preferred_element_type=f32)
    grad_proj_bias = jnp.sum(d_branch_one.astype(f32), axis=0)
    d_attn = jnp.einsum("rd,cd->rc", d_branch_one, proj_weight, preferred_element_type=f32).astype(
        bf16
    )
    d_attn = d_attn.reshape(images, length, heads_here, head_size)
    again_probs = jnp.exp(masked_scores() - log_total)
    again_low = again_probs.astype(bf16)
    d_probs = jnp.einsum("ishe,ithe->ihst", d_attn, value_low, preferred_element_type=f32)
    d_scores = (
        again_probs * (d_probs - jnp.sum(again_probs * d_probs, axis=-1, keepdims=True))
    ).astype(bf16)
    d_query_scaled = jnp.einsum("ihst,ithe->ishe", d_scores, key_low, preferred_element_type=f32)
    d_key_unit = jnp.einsum("ihst,ishe->ithe", d_scores, query_low, preferred_element_type=f32)
    d_value = jnp.einsum("ihst,ishe->ithe", again_low, d_attn, preferred_element_type=f32)
    grad_scale = jnp.sum(d_query_scaled * query_scaled, axis=(0, 1, 3))
    d_query_unit = d_query_scaled * growth
    d_query = query_inv * (
        d_query_unit - query_unit * jnp.sum(d_query_unit * query_unit, axis=-1, keepdims=True)
    )
    d_key = key_inv * (
        d_key_unit - key_unit * jnp.sum(d_key_unit * key_unit, axis=-1, keepdims=True)
    )
    d_qkv = (
        jnp.stack([d_query, d_key, d_value], axis=2).reshape(rows_all, 3, local_width).astype(bf16)
    )
    grad_q_bias = jnp.sum(d_qkv[:, 0].astype(f32), axis=0)
    grad_v_bias = jnp.sum(d_qkv[:, 2].astype(f32), axis=0)
    grad_qkv = jnp.einsum("rd,rpc->dpc", hidden_one, d_qkv, preferred_element_type=f32)
    d_hidden_one = tensor_sum(
        jnp.einsum("rpc,dpc->rd", d_qkv, qkv_weight, preferred_element_type=f32).astype(bf16)
    )
    d_hidden_one = d_hidden_one.reshape(images, length, model_width)
    d_inputs = d_middle + layer_back(d_hidden_one * (1.0 + scale_one), normed_one, inv_std_one)
    d_tokens = d_inputs.astype(bf16).reshape(rows_all, model_width)
    d_modul = jnp.concatenate(
        [
            jnp.sum(d_middle * branch_one, axis=1),
            jnp.sum(d_result * branch_two, axis=1),
            jnp.sum(d_hidden_one * normed_one, axis=1),
            jnp.sum(d_hidden_two * normed_two, axis=1),
            jnp.sum(d_hidden_one, axis=1),
            jnp.sum(d_hidden_two, axis=1),
        ],
        axis=1,
    ).astype(bf16)
    col_start = lax.axis_index("tensor") * mod_width
    dmod_cols = lax.dynamic_slice_in_dim(d_modul, col_start, mod_width, 1)
    dmod_all = lax.all_gather(dmod_cols, "dp", axis=0, tiled=True)
    small = [grad_q_bias, grad_v_bias, grad_scale, grad_proj_bias, grad_fc1_bias, grad_fc2_bias]
    sizes = [item.shape[0] for item in small]
    packed = lax.all_gather(jnp.concatenate(small), "dp", axis=0, tiled=False)
    packed = jnp.sum(packed, axis=0)
    ends = [sum(sizes[: k + 1]) for k in range(len(sizes))]
    grad_q_bias, grad_v_bias, grad_scale, grad_proj_bias, grad_fc1_bias, grad_fc2_bias = [
        packed[e - n : e] for e, n in zip(ends, sizes)
    ]
    act_all = jax.nn.silu(cond_all.astype(f32)).astype(bf16)
    d_act_part = jnp.einsum("ic,dc->id", dmod_all, ada_weight, preferred_element_type=f32)
    d_act_cols = lax.psum_scatter(d_act_part, "tensor", scatter_dimension=1, tiled=True)
    silu_value, silu_pull = jax.vjp(jax.nn.silu, cond_all_cols)
    d_cond = silu_pull(d_act_cols)[0]
    grad_table = jnp.einsum(
        "in,ic->nc", pick_all.astype(f32), d_cond, precision=highest, preferred_element_type=f32
    )
    grad_ada = jnp.einsum("id,ic->dc", act_all, dmod_all, preferred_element_type=f32)
    grad_ada_bias = jnp.sum(dmod_all.astype(f32), axis=0)
    grad_qkv, grad_proj, grad_fc1, grad_fc2 = (
        lax.psum(grad_qkv.astype(bf16), "dp").astype(f32),
        lax.psum(grad_proj.astype(bf16), "dp").astype(f32),
        lax.psum(grad_fc1.astype(bf16), "dp").astype(f32),
        lax.psum(grad_fc2.astype(bf16), "dp").astype(f32),
    )
    return (
        result,
        d_tokens,
        grad_table,
        grad_ada,
        grad_ada_bias,
        grad_qkv,
        grad_q_bias,
        grad_v_bias,
        grad_scale,
        grad_proj,
        grad_proj_bias,
        grad_fc1,
        grad_fc1_bias,
        grad_fc2,
        grad_fc2_bias,
    )


def solution(mesh):
    return jax.shard_map(
        per_device,
        mesh=mesh,
        in_specs=(
            P("dp", None),
            P("dp", None),
            P(),
            P("dp", None),
            P(None, "tensor"),
            P(None, "tensor"),
            P("tensor"),
            P(None, None, "tensor"),
            P("tensor"),
            P("tensor"),
            P("tensor"),
            P("tensor", None),
            P(),
            P(None, "tensor"),
            P("tensor"),
            P("tensor", None),
            P(),
        ),
        out_specs=(
            P("dp", None),
            P("dp", None),
            P(None, "tensor"),
            P(None, "tensor"),
            P("tensor"),
            P(None, None, "tensor"),
            P("tensor"),
            P("tensor"),
            P("tensor"),
            P("tensor", None),
            P(),
            P(None, "tensor"),
            P("tensor"),
            P("tensor", None),
            P(),
        ),
        check_vma=False,
    )
```

profile of v0, /device:TPU:0, one launch (start us, length us, event | category | flops | bytes accessed | tf_op | source)
XLA Modules:
  0.0 914.1 jit_solution(17370807732758407328)
XLA Ops:
  33.7 6.9 convolution_add_fusion
  40.6 12.9 %reshape.303 = f32[2,680,3,8,64]{4,3,1,0,2:T(8,128)} reshape(f32[1360,3,512]{2,0,1:T(8,128)} %convolution_add_fusion) | data formatting | bytes 16711680 | tf_op jit(solution)/shard_map/reshape | solution.py:82
  58.0 9.3 %fusion.104 = (f32[2,680,1,8,64]{4,3,1,0,2:T(8,128)}, f32[2,680,1,8,64]{4,3,1,0,2:T(8,128)}) fusion(f32[2,680,3,8,64]{4,3,1,0,2:T(8,128)} %reshape.303), kind=kLoop, calls=%fused_computation.175 | loop fusion | bytes 11141120 | tf_op jit(solution)/shard_map/slice | solution.py:83
  81.4 6.0 copy.107
  89.7 16.8 %select_reduce_fusion = (f32[2,8,680]{2,1,0:T(8,128)S(1)}, f32[2,8,680,680]{2,3,1,0:T(8,128)}) fusion(pred[2,680,680]{1,2,0:T(8,128)(4,1)} %broadcast_compare_fusion, f32[2,680,1,8,64]{1,4,3,0,2:T(8,128)} %copy.107, f32[2,680,8]{1,2,0:T(8,128)S(1)} %get-tuple-element.67, f32[2,680,1,8,64]{1,4,3,0,2:T(8,128)} %copy.106, f32[8]{0:T(128)S(1)} %exp.22, ...), kind=kOutput, calls=%fused_computation.8 | convolution fusion | flops 965262720 | bytes 36219552 | tf_op jit(solution)/shard_map/ishe,ithe->ihst/dot_general | solution.py:98
  106.5 14.0 %fusion.2 = f32[2,8,680]{2,1,0:T(8,128)S(1)} fusion(f32[2,8,680,680]{2,3,1,0:T(8,128)} %get-tuple-element.62, f32[2,8,680]{2,1,0:T(8,128)S(1)} %get-tuple-element.61, pred[2,680,680]{1,2,0:T(8,128)(4,1)S(1)} %copy-done.8), kind=kLoop, calls=%fused_computation.7 | loop fusion | flops 22184320 | bytes 30605440 | tf_op jit(solution)/shard_map/reduce_sum | solution.py:104
  120.5 16.6 %fusion.51 = bf16[2,680,8,64]{1,3,2,0:T(8,128)(2,1)} fusion(f32[2,8,680,680]{2,3,1,0:T(8,128)} %get-tuple-element.62, f32[2,8,680]{2,1,0:T(8,128)S(1)} %fusion.2, f32[2,8,680]{2,1,0:T(8,128)S(1)} %get-tuple-element.61, pred[2,680,680]{1,2,0:T(8,128)(4,1)S(1)} %copy-done.8, bf16[2,680,1,8,64]{1,4,3,0,2:T(8,128)(2,1)} %copy.105), kind=kOutput, calls=%fused_computation.104 | convolution fusion | flops 977285120 | bytes 33390720 | tf_op jit(solution)/shard_map/ihst,ithe->ishe/dot_general | solution.py:108
  159.3 52.3 %collective-permute-done = bf16[1360,1024]{1,0:T(8,128)(2,1)} collective-permute-done((bf16[1360,1024]{1,0:T(8,128)(2,1)}, bf16[1360,1024]{1,0:T(8,128)(2,1)}, u32[]{:S(2)}, u32[]{:S(2)}) %collective-permute-start) | collective-permute-done | bytes 2785312 | tf_op jit(solution)/shard_map/ppermute | solution.py:13
  211.6 6.6 bitcast_multiply_fusion.3
  222.9 8.7 fusion.108
  231.7 11.3 %convolution_convert_fusion.1 = bf16[1360,1024]{1,0:T(8,128)(2,1)} fusion(bf16[2048,1024]{1,0:T(8,128)(2,1)S(1)} %copy-done.45, f32[1360,2048]{1,0:T(8,128)} %fusion.108, f32[2048]{0:T(1024)S(1)} %convert_element_type.198), kind=kOutput, calls=%fused_computation.63 | convolution fusion | flops 5733498880 | bytes 18128896 | tf_op jit(solution)/shard_map/dot_general | solution.py:123
  244.8 16.8 %convert_reduce_fusion = (f32[2048]{0:T(1024)}, bf16[1360,2048]{1,0:T(8,128)(2,1)}) fusion(f32[1360,2048]{1,0:T(8,128)} %fusion.108, f32[2048]{0:T(1024)S(1)} %convert_element_type.198, bf16[1360,1024]{1,0:T(8,128)(2,1)S(1)} %get-tuple-element.30, bf16[2048,1024]{1,0:T(8,128)(2,1)S(1)} %copy-done.45), kind=kOutput, calls=%fused_computation.24 | convolution fusion | flops 5768312832 | bytes 23707648 | tf_op jit(solution)/shard_map/rd,fd->rf/dot_general | solution.py:129
  261.6 10.0 %convolution_convert_fusion = bf16[1360,1024]{1,0:T(8,128)(2,1)} fusion(bf16[1360,2048]{1,0:T(8,128)(2,1)} %get-tuple-element.32, bf16[1024,2048]{1,0:T(8,128)(2,1)S(1)} %copy-done.46), kind=kOutput, calls=%fused_computation.62 | convolution fusion | flops 5705646080 | bytes 12550144 | tf_op jit(solution)/shard_map/rf,df->rd/dot_general | solution.py:135
  271.9 12.8 %convolution_convert_fusion.2 = bf16[2048,1024]{1,0:T(8,128)(2,1)} fusion(bf16[1360,1024]{1,0:T(8,128)(2,1)S(1)} %get-tuple-element.30, f32[1360,2048]{1,0:T(8,128)} %fusion.108, f32[2048]{0:T(1024)S(1)} %convert_element_type.198), kind=kOutput, calls=%fused_computation.64 | convolution fusion | flops 5734203392 | bytes 18128896 | tf_op jit(solution)/shard_map/rf,rd->fd/dot_general | solution.py:127
  284.9 77.4 %collective-permute-done.2 = bf16[1360,1024]{1,0:T(8,128)(2,1)} collective-permute-done((bf16[1360,1024]{1,0:T(8,128)(2,1)}, bf16[1360,1024]{1,0:T(8,128)(2,1)}, u32[]{:S(2)}, u32[]{:S(2)}) %collective-permute-start.2) | collective-permute-done | bytes 2785312 | tf_op jit(solution)/shard_map/ppermute | solution.py:13
  365.5 7.7 fusion.99
  373.3 12.9 %convert_reduce_fusion.2 = (f32[1024]{0:T(1024)S(1)}, bf16[1360,1024]{1,0:T(8,128)(2,1)}, f32[1360,1024]{1,0:T(8,128)}, f32[1360,1024]{1,0:T(8,128)}, bf16[1360,1024]{1,0:T(8,128)(2,1)}, /*index=5*/f32[1360,1024]{1,0:T(8,128)}) fusion(f32[2,1024]{1,0:T(2,128)S(1)} %get-tuple-element.54, f32[1360]{0:T(1024)S(1)} %broadcast_multiply_fusion.2, ...), kind=kLoop, calls=%fused_computation.40 | loop fusion | flops 32029696 | bytes 41833728 | tf_op jit(solution)/shard_map/reduce_sum | solution.py:141
  399.4 16.6 %fusion.48 = bf16[2,680,8,64]{1,3,2,0:T(8,128)(2,1)} fusion(bf16[2,680,8,64]{1,3,2,0:T(8,128)(2,1)} %copy.84, f32[2,8,680,680]{2,3,1,0:T(8,128)} %get-tuple-element.62, f32[2,8,680]{2,1,0:T(8,128)S(1)} %log_add_fusion, pred[2,680,680]{1,2,0:T(8,128)(4,1)} %broadcast_compare_fusion), kind=kOutput, calls=%fused_computation.102 | convolution fusion | flops 969886720 | bytes 33347200 | tf_op jit(solution)/shard_map/ihst,ishe->ithe/dot_general | solution.py:154
  416.1 30.7 %multiply_reduce_fusion = (f32[2,8,680]{2,1,0:T(8,128)S(1)}, f32[2,8,680,680]{2,3,1,0:T(8,128)}) fusion(f32[2,8,680,680]{2,3,1,0:T(8,128)} %get-tuple-element.62, f32[2,8,680]{2,1,0:T(8,128)S(1)} %log_add_fusion, pred[2,680,680]{1,2,0:T(8,128)(4,1)} %broadcast_compare_fusion, bf16[2,680,8,64]{1,3,2,0:T(8,128)(2,1)} %copy.84, ...), kind=kOutput, calls=%fused_computation.3 | convolution fusion | flops 976577920 | bytes 62984320 | tf_op jit(solution)/shard_map/ishe,ithe->ihst/dot_general | solution.py:148
  446.8 28.4 %multiply_convert_fusion = bf16[2,8,680,680]{2,3,1,0:T(8,128)(2,1)} fusion(f32[2,8,680,680]{2,3,1,0:T(8,128)} %get-tuple-element.64, f32[2,8,680,680]{2,3,1,0:T(8,128)} %get-tuple-element.62, f32[2,8,680]{2,1,0:T(8,128)S(1)} %get-tuple-element.63, f32[2,8,680]{2,1,0:T(8,128)S(1)} %log_add_fusion, pred[2,680,680]{1,2,0:T(8,128)(4,1)} %broadcast_compare_fusion), kind=kLoop, calls=%fused_computation.2 | loop fusion | flops 36992000 | bytes 74995840 | tf_op jit(solution)/shard_map/convert_element_type | solution.py:151
  475.2 11.5 %fusion.97 = f32[2,8,64,680]{3,2,1,0:T(8,128)} fusion(bf16[2,8,680,680]{2,3,1,0:T(8,128)(2,1)} %multiply_convert_fusion, f32[2,680,1,8,64]{1,4,3,0,2:T(8,128)} %copy.106, f32[8]{0:T(128)S(1)} %copy-done.31, f32[2,680,8]{1,2,0:T(8,128)S(1)} %copy-done.12), kind=kOutput, calls=%fused_computation.171 | convolution fusion | flops 949084160 | bytes 20410912 | tf_op jit(solution)/shard_map/ihst,ishe->ithe/dot_general | solution.py:153
  486.7 10.5 %fusion.25 = (f32[8]{0:T(128)S(1)}, f32[2,8,64,680]{3,2,1,0:T(8,128)}) fusion(f32[2,680,1,8,64]{1,4,3,0,2:T(8,128)S(1)} %copy-done.5, f32[8]{0:T(128)S(1)} %copy-done.31, f32[2,680,8]{1,2,0:T(8,128)S(1)} %copy-done.12, bf16[2,8,680,680]{2,3,1,0:T(8,128)(2,1)} %multiply_convert_fusion, f32[2,680,1,8,64]{1,4,3,0,2:T(8,128)S(1)} %copy-done.7, ...), kind=kOutput, calls=%fused_computation.74 | convolution fusion | flops 951173120 | bytes 23239744 | tf_op jit(solution)/shard_map/ihst,ithe->ishe/dot_general | solution.py:152
  507.2 6.8 fusion.24
  534.1 8.2 bitcast_convert_fusion
  543.7 11.0 %convolution_convert_fusion.3 = bf16[1024,2048]{1,0:T(8,128)(2,1)} fusion(bf16[1360,1024]{1,0:T(8,128)(2,1)S(1)} %copy-done.17, bf16[1360,2048]{1,0:T(8,128)(2,1)} %get-tuple-element.32), kind=kOutput, calls=%fused_computation.65 | convolution fusion | flops 5706350592 | bytes 12550144 | tf_op jit(solution)/shard_map/rd,rf->df/dot_general | solution.py:132
  559.6 9.5 %fusion.35 = bf16[1024,3,512]{2,0,1:T(8,128)(2,1)} fusion(bf16[1360,1024]{1,0:T(8,128)(2,1)} %copy-done.15, bf16[1360,1,512]{2,0,1:T(8,128)(2,1)} %copy.94, bf16[1360,1,512]{2,0,1:T(8,128)(2,1)} %reshape.302, bf16[1360,1,512]{2,0,1:T(8,128)(2,1)} %copy.92), kind=kOutput, calls=%fused_computation.92 | convolution fusion | flops 4292296704 | bytes 10108928 | tf_op jit(solution)/shard_map/rd,rpc->dpc/dot_general | solution.py:168
  569.1 31.9 %collective-permute-done.3 = bf16[1360,1024]{1,0:T(8,128)(2,1)} collective-permute-done((bf16[1360,1024]{1,0:T(8,128)(2,1)}, bf16[1360,1024]{1,0:T(8,128)(2,1)}, u32[]{:S(2)}, u32[]{:S(2)}) %collective-permute-start.3) | collective-permute-done | bytes 2785312 | tf_op jit(solution)/shard_map/ppermute | solution.py:13
  604.2 6.5 fusion.98
  616.3 9.5 %multiply_reduce_fusion.1 = (bf16[2,1024]{1,0:T(2,128)(2,1)S(1)}, bf16[2,1024]{1,0:T(2,128)(2,1)S(1)}, bf16[2,1024]{1,0:T(2,128)(2,1)S(1)}, bf16[2,1024]{1,0:T(2...) fusion(f32[2,680,1024]{2,1,0:T(8,128)} %bitcast.179, f32[2,680,1024]{2,1,0:T(8,128)S(1)} %bitcast.178, ...), kind=kLoop, calls=%fused_computation.41 | loop fusion | flops 33411072 | bytes 27926400 | tf_op jit(solution)/shard_map/reduce_sum | solution.py:180
  625.9 21.9 %all-gather.1 = bf16[16,2,3072]{2,1,0:T(2,128)(2,1)S(1)} all-gather(bf16[1,2,3072]{2,1,0:T(2,128)(2,1)S(1)} %dynamic-slice_bitcast_fusion), channel_id=1, replica_groups=mesh['dp'=16,'tensor'=2] {'dp'}, dimensions={0}, use_global_device_ids=true | all-gather | bytes 208896 | tf_op jit(solution)/shard_map/all_gather | solution.py:188
  664.8 6.6 fusion.66
  674.6 214.2 %all-reduce.7.cloned.1.call-done = (bf16[1024,3,512]{2,0,1:T(8,128)(2,1)}, bf16[512,1024]{1,0:T(8,128)(2,1)}, bf16[1024,2048]{1,0:T(8,128)(2,1)}, bf16[2048,1024]{1,0:T(8,128)(2,1)}) async-done(((bf16[1024,3,512]{2,0,1:T(8,128)(2,1)}, bf16[512,1024]{1,0:T(8,128)(2,1)}, bf16[1024,2048]{1,0:T(8,128)(2,1)}, bf16[2048,1024]{1,0:T(8,128)(2,1)}), (bf16[1024,3,512]{2,0,1:T(8,128)(2,1)}, ...) | async-done | bytes 12582928 | tf_op jit(solution)/shard_map/psum | solution.py:208
  (217 shorter events, 174.1 us)
Async XLA Ops:
  8.0 25.7 %copy-start = (bf16[1024,3,512]{2,0,1:T(8,128)(2,1)S(1)}, bf16[1024,3,512]{2,0,1:T(8,128)(2,1)}, u32[]{:S(2)}) copy-start(bf16[1024,3,512]{2,0,1:T(8,128)(2,1)} %param.24) | copy-start | bytes 9437188
  8.1 650.7 %all-reduce.5.cloned.1.call-start = ((), (), s32[]{:S(2)}) async-start(), calls=%async_computation.2 | async-start | bytes 663552
  12.0 141.3 %copy-start.25 = (f32[1360]{0:T(1024)}, f32[1360]{0:T(1024)S(1)}, u32[]{:S(2)}) copy-start(f32[1360]{0:T(1024)S(1)} %broadcast_multiply_fusion.5) | copy-start | bytes 16324
  14.7 139.2 %copy-start.28 = (f32[1360]{0:T(1024)}, f32[1360]{0:T(1024)S(1)}, u32[]{:S(2)}) copy-start(f32[1360]{0:T(1024)S(1)} %add_rsqrt_fusion.3) | copy-start | bytes 16324
  21.2 11.1 %copy-start.23 = (bf16[32,1024]{1,0:T(8,128)(2,1)}, bf16[32,1024]{1,0:T(8,128)(2,1)S(1)}, u32[]{:S(2)}) copy-start(bf16[32,1024]{1,0:T(8,128)(2,1)S(1)} %all_gather.15) | copy-start | bytes 196612
  29.5 11.1 %copy-start.32 = (f32[2,1024]{1,0:T(2,128)}, f32[2,1024]{1,0:T(2,128)S(1)}, u32[]{:S(2)}) copy-start(f32[2,1024]{1,0:T(2,128)S(1)} %get-tuple-element.53) | copy-start | bytes 24580
  67.3 22.4 %copy-start.30 = (f32[8]{0:T(128)}, f32[8]{0:T(128)S(1)}, u32[]{:S(2)}) copy-start(f32[8]{0:T(128)S(1)} %exp.22) | copy-start | bytes 100
  89.6 16.8 %copy-start.11 = (f32[2,680,8]{1,2,0:T(8,128)}, f32[2,680,8]{1,2,0:T(8,128)S(1)}, u32[]{:S(2)}) copy-start(f32[2,680,8]{1,2,0:T(8,128)S(1)} %get-tuple-element.68) | copy-start | bytes 130564
  89.6 16.8 %copy-start.18 = (f32[2,680,8]{1,2,0:T(8,128)}, f32[2,680,8]{1,2,0:T(8,128)S(1)}, u32[]{:S(2)}) copy-start(f32[2,680,8]{1,2,0:T(8,128)S(1)} %get-tuple-element.67) | copy-start | bytes 130564
  89.7 16.8 %copy-start.8 = (pred[2,680,680]{1,2,0:T(8,128)(4,1)S(1)}, pred[2,680,680]{1,2,0:T(8,128)(4,1)}, u32[]{:S(2)}) copy-start(pred[2,680,680]{1,2,0:T(8,128)(4,1)} %broadcast_compare_fusion) | copy-start | bytes 2774404
  151.2 60.4 %collective-permute-start = (bf16[1360,1024]{1,0:T(8,128)(2,1)}, bf16[1360,1024]{1,0:T(8,128)(2,1)}, u32[]{:S(2)}, u32[]{:S(2)}) collective-permute-start(bf16[1360,1024]{1,0:T(8,128)(2,1)} %convolution_convert_fusion.4), channel_id=1, source_target_pairs={{0,1},{1,0},{2,3},{3,2},{4,5},{5,4},{6,7},{7,6},{8,9},{9,8},{10,11... | collective-permute-start | bytes 8355848 | tf_op jit(solution)/shard_map/ppermute | solution.py:13
  243.0 130.2 %collective-permute-start.1 = (bf16[1360,1024]{1,0:T(8,128)(2,1)}, bf16[1360,1024]{1,0:T(8,128)(2,1)}, u32[]{:S(2)}, u32[]{:S(2)}) collective-permute-start(bf16[1360,1024]{1,0:T(8,128)(2,1)} %convolution_convert_fusion.1), channel_id=1, source_target_pairs={{0,1},{1,0},{2,3},{3,2},{4,5},{5,4},{6,7},{7,6},{8,9},{9,8},{10,11... | collective-permute-start | bytes 8355848 | tf_op jit(solution)/shard_map/ppermute | solution.py:13
  271.6 90.7 %collective-permute-start.2 = (bf16[1360,1024]{1,0:T(8,128)(2,1)}, bf16[1360,1024]{1,0:T(8,128)(2,1)}, u32[]{:S(2)}, u32[]{:S(2)}) collective-permute-start(bf16[1360,1024]{1,0:T(8,128)(2,1)} %convolution_convert_fusion), channel_id=1, source_target_pairs={{0,1},{1,0},{2,3},{3,2},{4,5},{5,4},{6,7},{7,6},{8,9},{9,8},{10,11... | collective-permute-start | bytes 8355848 | tf_op jit(solution)/shard_map/ppermute | solution.py:13
  362.3 11.0 %slice-start = ((s8[5570560]{0:T(1024)(128)(4,1)}), s8[4194304]{0:T(1024)(128)(4,1)S(1)}, s32[]{:S(2)}) async-start(s8[5570560]{0:T(1024)(128)(4,1)} %bitcast.169), calls=%async_computation.4 | async-start | bytes 8388608
  373.2 12.9 %copy-start.47 = (bf16[512,1024]{1,0:T(8,128)(2,1)S(1)}, bf16[512,1024]{1,0:T(8,128)(2,1)}, u32[]{:S(2)}) copy-start(bf16[512,1024]{1,0:T(8,128)(2,1)} %param.28) | copy-start | bytes 3145732
  446.8 28.4 %copy-start.12 = (f32[2,680,8]{1,2,0:T(8,128)S(1)}, f32[2,680,8]{1,2,0:T(8,128)}, u32[]{:S(2)}) copy-start(f32[2,680,8]{1,2,0:T(8,128)} %copy-done.11) | copy-start | bytes 130564
  446.8 28.4 %copy-start.31 = (f32[8]{0:T(128)S(1)}, f32[8]{0:T(128)}, u32[]{:S(2)}) copy-start(f32[8]{0:T(128)} %copy-done.30) | copy-start | bytes 100
  475.2 11.5 %copy-start.5 = (f32[2,680,1,8,64]{1,4,3,0,2:T(8,128)S(1)}, f32[2,680,1,8,64]{1,4,3,0,2:T(8,128)}, u32[]{:S(2)}) copy-start(f32[2,680,1,8,64]{1,4,3,0,2:T(8,128)} %copy.106) | copy-start | bytes 8355844
  475.2 11.5 %copy-start.7 = (f32[2,680,1,8,64]{1,4,3,0,2:T(8,128)S(1)}, f32[2,680,1,8,64]{1,4,3,0,2:T(8,128)}, u32[]{:S(2)}) copy-start(f32[2,680,1,8,64]{1,4,3,0,2:T(8,128)} %copy.107) | copy-start | bytes 8355844
  475.2 11.5 %copy-start.19 = (f32[2,680,8]{1,2,0:T(8,128)S(1)}, f32[2,680,8]{1,2,0:T(8,128)}, u32[]{:S(2)}) copy-start(f32[2,680,8]{1,2,0:T(8,128)} %copy-done.18) | copy-start | bytes 130564
  486.7 10.5 %copy-start.20 = (bf16[2,680,8,64]{1,3,2,0:T(8,128)(2,1)S(1)}, bf16[2,680,8,64]{1,3,2,0:T(8,128)(2,1)}, u32[]{:S(2)}) copy-start(bf16[2,680,8,64]{1,3,2,0:T(8,128)(2,1)} %fusion.48) | copy-start | bytes 4177924
  542.3 15.9 %copy-start.37 = (f32[1024]{0:T(1024)S(1)}, f32[1024]{0:T(1024)}, u32[]{:S(2)}) copy-start(f32[1024]{0:T(1024)} %get-tuple-element.29) | copy-start | bytes 12292
  542.3 15.9 %copy-start.38 = (f32[2048]{0:T(1024)S(1)}, f32[2048]{0:T(1024)}, u32[]{:S(2)}) copy-start(f32[2048]{0:T(1024)} %get-tuple-element.31) | copy-start | bytes 24580
  542.3 58.7 %collective-permute-start.3 = (bf16[1360,1024]{1,0:T(8,128)(2,1)}, bf16[1360,1024]{1,0:T(8,128)(2,1)}, u32[]{:S(2)}, u32[]{:S(2)}) collective-permute-start(bf16[1360,1024]{1,0:T(8,128)(2,1)} %bitcast_convert_fusion), channel_id=1, source_target_pairs={{0,1},{1,0},{2,3},{3,2},{4,5},{5,4},{6,7},{7,6},{8,9},{9,8},{10,11... | collective-permute-start | bytes 8355848 | tf_op jit(solution)/shard_map/ppermute | solution.py:13
  559.5 41.4 %copy-start.33 = (f32[2,1024]{1,0:T(2,128)S(1)}, f32[2,1024]{1,0:T(2,128)}, u32[]{:S(2)}) copy-start(f32[2,1024]{1,0:T(2,128)} %copy-done.32) | copy-start | bytes 24580
  559.5 111.9 %reduce-scatter.2.cloned.1.call-start = ((), (), s32[]{:S(2)}) async-start(), calls=%async_computation.1 | async-start | bytes 196608 | tf_op jit(solution)/shard_map/reduce_scatter | solution.py:199
  569.1 35.1 %copy-start.4 = (bf16[1360,1024]{1,0:T(8,128)(2,1)S(1)}, bf16[1360,1024]{1,0:T(8,128)(2,1)}, u32[]{:S(2)}) copy-start(bf16[1360,1024]{1,0:T(8,128)(2,1)} %param.17) | copy-start | bytes 8355844
  569.1 35.1 %copy-start.26 = (f32[1360]{0:T(1024)S(1)}, f32[1360]{0:T(1024)}, u32[]{:S(2)}) copy-start(f32[1360]{0:T(1024)} %copy-done.25) | copy-start | bytes 16324
  569.1 35.1 %copy-start.29 = (f32[1360]{0:T(1024)S(1)}, f32[1360]{0:T(1024)}, u32[]{:S(2)}) copy-start(f32[1360]{0:T(1024)} %copy-done.28) | copy-start | bytes 16324
  600.9 9.8 %slice-start.2 = ((s8[5570560]{0:T(1024)(128)(4,1)}), s8[4194304]{0:T(1024)(128)(4,1)S(1)}, s32[]{:S(2)}) async-start(s8[5570560]{0:T(1024)(128)(4,1)} %bitcast.174), calls=%async_computation.6 | async-start | bytes 8388608
  604.2 12.1 %slice-start.4 = ((s8[5570560]{0:T(1024)(128)(4,1)}), s8[4194304]{0:T(1024)(128)(4,1)S(1)}, s32[]{:S(2)}) async-start(s8[5570560]{0:T(1024)(128)(4,1)} %bitcast.176), calls=%async_computation.8 | async-start | bytes 8388608
  653.3 235.5 %all-reduce.7.cloned.1.call-start = ((), (), s32[]{:S(2)}) async-start(), calls=%async_computation.3 | async-start | bytes 25165824 | tf_op jit(solution)/shard_map/psum | solution.py:208
  (31 other events, 204.8 us)
Sparse Core Ops, SparseCore 0:
  559.6 89.7 all-reduce.4
  659.3 229.5 all-reduce.6
Sparse Core Ops, SparseCore 1:
  653.4 7.6 reduce-scatter.1
where the time goes:
time: 920 us; the launch traced here: 914 us
  waiting for transfers between devices  376 us (41%)
  matrix products  232 us (25%)
  other arithmetic  144 us (16%)
  local copies, waits for them, and re-layouts  107 us (12%)
  blocking collectives  31.9 us (3%)
  between operations  17.4 us (2%)
    psum x1, waiting for transfers between devices, per_device(): lax.psum(grad_qkv.astype(bf16), 'dp').astype(f32)  214 us
    ppermute x4, waiting for transfers between devices, tensor_sum(): other = lax.ppermute(part, 'tensor', [(0, 1), (1, 0)])  162 us
    dot_general x1, matrix products, per_device(): jnp.einsum('ishe,ithe->ihst', d_attn, value_low, preferred_element_type=f32)  30.7 us
    convert_element_type x1, other arithmetic, per_device(): d_scores = (again_probs * (d_probs - jnp.sum(again_probs * d_probs, axis=...  28.4 us
    another operation x6, local copies, waits for them, and re-layouts, per_device(): jnp.stack([d_query, d_key, d_value], axis=2)  23.5 us
    all_gather x1, blocking collectives, per_device(): dmod_all = lax.all_gather(dmod_cols, 'dp', axis=0, tiled=True)  21.9 us
    unnamed x125, local copies, waits for them, and re-layouts  20.8 us
  transfers between devices with their start and end apart: 7, of which 4 were waited for; matrix products, arithmetic and copies ran while one was open for 14% of the time, Pallas kernels for 0%

commit v1 on v0

--- a/solution.py
+++ b/solution.py
@@ -3,6 +3,7 @@
 import jax.numpy as jnp
 from jax import lax
 from jax.sharding import PartitionSpec as P
+from jax.lax import axis_index, ppermute, psum
 
 epsilon = 1e-06
 highest = lax.Precision.HIGHEST
@@ -185,7 +186,24 @@
     ).astype(bf16)
     col_start = lax.axis_index("tensor") * mod_width
     dmod_cols = lax.dynamic_slice_in_dim(d_modul, col_start, mod_width, 1)
-    dmod_all = lax.all_gather(dmod_cols, "dp", axis=0, tiled=True)
+    v_next, known, carry_in = (psum(1, axis_name="dp"), axis_index("dp"), dmod_cols.shape[0])
+    rack = [jj * v_next if j0 == 0 else jj for j0, jj in enumerate(dmod_cols.shape)]
+    y2 = mixed_arr = dmod_cols
+    dmod_all = lax.dynamic_update_slice_in_dim(
+        jnp.zeros(rack, dmod_cols.dtype), dmod_cols, known * carry_in, axis=0
+    )
+    for c in range(1, v_next // 2 + 1):
+        y2 = ppermute(y2, axis_name="dp", perm=[(j0, (j0 + 1) % v_next) for j0 in range(v_next)])
+        dmod_all = lax.dynamic_update_slice_in_dim(
+            dmod_all, y2, (known - c) % v_next * carry_in, axis=0
+        )
+        if 2 * c < v_next:
+            mixed_arr = ppermute(
+                mixed_arr, axis_name="dp", perm=[(j0, (j0 - 1) % v_next) for j0 in range(v_next)]
+            )
+            dmod_all = lax.dynamic_update_slice_in_dim(
+                dmod_all, mixed_arr, (known + c) % v_next * carry_in, axis=0
+            )
     small = [grad_q_bias, grad_v_bias, grad_scale, grad_proj_bias, grad_fc1_bias, grad_fc2_bias]
     sizes = [item.shape[0] for item in small]
     packed = lax.all_gather(jnp.concatenate(small), "dp", axis=0, tiled=False)

time: 920 us -> 991 us (1.077)
  waiting for transfers between devices: 376 us -> 437 us
  starting transfers between devices: 5.94 us -> 37.1 us
  blocking collectives: 31.9 us -> 9.99 us
    unnamed x4, waiting for transfers between devices: 0.07 us -> 36.3 us
    ppermute x0 -> x15, starting transfers between devices: none -> 31.2 us  [the longest x7 31.1 us: per_device(): ppermute(mixed_arr, axis_name='dp', perm=[(j0, (j0 - 1) % v_next) for j0...]
    all_gather x1 -> x0, blocking collectives: 21.9 us -> none  [per_device(): dmod_all = lax.all_gather(dmod_cols, 'dp', axis=0, tiled=True)]
    ppermute x0 -> x15, waiting for transfers between devices: none -> 13.7 us  [the longest x8 13.4 us: per_device(): ppermute(y2, axis_name='dp', perm=[(j0, (j0 + 1) % v_next) for j0 in rang...]
    unnamed x125 -> x123, local copies, waits for them, and re-layouts: 20.8 us -> 21.7 us
  transfers between devices with their start and end apart: 7 -> 22, of which waited for: 4 -> 16; matrix products, arithmetic and copies ran while one was open for 14% -> 11% of each run, Pallas kernels for 0% -> 0%
where the time goes in v1:
time: 991 us; the launch traced here: 985 us
  waiting for transfers between devices  437 us (44%)
  matrix products  233 us (24%)
  other arithmetic  142 us (14%)
  local copies, waits for them, and re-layouts  108 us (11%)
  starting transfers between devices  37.1 us (4%)
  between operations  17.3 us (2%)
  blocking collectives  9.99 us (1%)
    psum x1, waiting for transfers between devices, per_device(): lax.psum(grad_qkv.astype(bf16), 'dp').astype(f32)  222 us
    ppermute x4, waiting for transfers between devices, tensor_sum(): other = lax.ppermute(part, 'tensor', [(0, 1), (1, 0)])  164 us
    unnamed x4, waiting for transfers between devices  36.3 us
    ppermute x7, starting transfers between devices, per_device(): ppermute(mixed_arr, axis_name='dp', perm=[(j0, (j0 - 1) % v_next) for j0...  31.1 us
    dot_general x1, matrix products, per_device(): jnp.einsum('ishe,ithe->ihst', d_attn, value_low, preferred_element_type=f32)  30.9 us
    convert_element_type x1, other arithmetic, per_device(): d_scores = (again_probs * (d_probs - jnp.sum(again_probs * d_probs, axis=...  28.4 us
    another operation x6, local copies, waits for them, and re-layouts, per_device(): jnp.stack([d_query, d_key, d_value], axis=2)  23.7 us
    unnamed x123, local copies, waits for them, and re-layouts  21.7 us
  transfers between devices with their start and end apart: 22, of which 16 were waited for; matrix products, arithmetic and copies ran while one was open for 11% of the time, Pallas kernels for 0%

profile of v1, /device:TPU:0, one launch (start us, length us, event | category | flops | bytes accessed | tf_op | source)
XLA Modules:
  0.0 984.9 jit_solution(6672144057323604511)
XLA Ops:
  33.7 7.0 convolution_add_fusion
  40.7 12.8 %reshape.301 = f32[2,680,3,8,64]{4,3,1,0,2:T(8,128)} reshape(f32[1360,3,512]{2,0,1:T(8,128)} %convolution_add_fusion) | data formatting | bytes 16711680 | tf_op jit(solution)/shard_map/reshape | solution.py:83
  58.1 9.3 fusion.102
  81.4 5.9 copy.89
  89.6 16.9 %select_reduce_fusion = (f32[2,8,680]{2,1,0:T(8,128)S(1)}, f32[2,8,680,680]{2,3,1,0:T(8,128)}) fusion(pred[2,680,680]{1,2,0:T(8,128)(4,1)} %broadcast_compare_fusion, f32[2,680,1,8,64]{1,4,3,0,2:T(8,128)} %copy.89, f32[2,680,8]{1,2,0:T(8,128)S(1)} %get-tuple-element.69, f32[2,680,1,8,64]{1,4,3,0,2:T(8,128)} %copy.88, f32[8]{0:T(128)S(1)} %exp.22, ...), kind=kOutput, calls=%fused_computation.8 | convolution fusion | flops 965262720 | bytes 36219552 | tf_op jit(solution)/shard_map/ishe,ithe->ihst/dot_general | solution.py:99
  106.6 14.0 %fusion.2 = f32[2,8,680]{2,1,0:T(8,128)S(1)} fusion(f32[2,8,680,680]{2,3,1,0:T(8,128)} %get-tuple-element.64, f32[2,8,680]{2,1,0:T(8,128)S(1)} %get-tuple-element.63, pred[2,680,680]{1,2,0:T(8,128)(4,1)S(1)} %copy-done.8), kind=kLoop, calls=%fused_computation.7 | loop fusion | flops 22184320 | bytes 30605440 | tf_op jit(solution)/shard_map/reduce_sum | solution.py:105
  120.6 16.8 %fusion.51 = bf16[2,680,8,64]{1,3,2,0:T(8,128)(2,1)} fusion(f32[2,8,680,680]{2,3,1,0:T(8,128)} %get-tuple-element.64, f32[2,8,680]{2,1,0:T(8,128)S(1)} %fusion.2, f32[2,8,680]{2,1,0:T(8,128)S(1)} %get-tuple-element.63, pred[2,680,680]{1,2,0:T(8,128)(4,1)S(1)} %copy-done.8, bf16[2,680,1,8,64]{1,4,3,0,2:T(8,128)(2,1)} %copy.87), kind=kOutput, calls=%fused_computation.104 | convolution fusion | flops 977285120 | bytes 33390720 | tf_op jit(solution)/shard_map/ihst,ithe->ishe/dot_general | solution.py:109
  159.4 52.2 %collective-permute-done = bf16[1360,1024]{1,0:T(8,128)(2,1)} collective-permute-done((bf16[1360,1024]{1,0:T(8,128)(2,1)}, bf16[1360,1024]{1,0:T(8,128)(2,1)}, u32[]{:S(2)}, u32[]{:S(2)}) %collective-permute-start) | collective-permute-done | bytes 2785312 | tf_op jit(solution)/shard_map/ppermute | solution.py:14
  211.7 6.6 bitcast_multiply_fusion.3
  223.0 8.7 fusion.106
  231.8 11.4 %convolution_convert_fusion.1 = bf16[1360,1024]{1,0:T(8,128)(2,1)} fusion(bf16[2048,1024]{1,0:T(8,128)(2,1)S(1)} %copy-done.45, f32[1360,2048]{1,0:T(8,128)} %fusion.106, f32[2048]{0:T(1024)S(1)} %convert_element_type.198), kind=kOutput, calls=%fused_computation.63 | convolution fusion | flops 5733498880 | bytes 18128896 | tf_op jit(solution)/shard_map/dot_general | solution.py:124
  244.9 16.8 %convert_reduce_fusion = (f32[2048]{0:T(1024)}, bf16[1360,2048]{1,0:T(8,128)(2,1)}) fusion(f32[1360,2048]{1,0:T(8,128)} %fusion.106, f32[2048]{0:T(1024)S(1)} %convert_element_type.198, bf16[1360,1024]{1,0:T(8,128)(2,1)S(1)} %get-tuple-element.30, bf16[2048,1024]{1,0:T(8,128)(2,1)S(1)} %copy-done.45), kind=kOutput, calls=%fused_computation.24 | convolution fusion | flops 5768312832 | bytes 23707648 | tf_op jit(solution)/shard_map/rd,fd->rf/dot_general | solution.py:130
  261.7 10.0 %convolution_convert_fusion = bf16[1360,1024]{1,0:T(8,128)(2,1)} fusion(bf16[1360,2048]{1,0:T(8,128)(2,1)} %get-tuple-element.32, bf16[1024,2048]{1,0:T(8,128)(2,1)S(1)} %copy-done.46), kind=kOutput, calls=%fused_computation.62 | convolution fusion | flops 5705646080 | bytes 12550144 | tf_op jit(solution)/shard_map/rf,df->rd/dot_general | solution.py:136
  272.0 13.1 %convolution_convert_fusion.2 = bf16[2048,1024]{1,0:T(8,128)(2,1)} fusion(bf16[1360,1024]{1,0:T(8,128)(2,1)S(1)} %get-tuple-element.30, f32[1360,2048]{1,0:T(8,128)} %fusion.106, f32[2048]{0:T(1024)S(1)} %convert_element_type.198), kind=kOutput, calls=%fused_computation.64 | convolution fusion | flops 5734203392 | bytes 18128896 | tf_op jit(solution)/shard_map/rf,rd->fd/dot_general | solution.py:128
  285.2 77.2 %collective-permute-done.2 = bf16[1360,1024]{1,0:T(8,128)(2,1)} collective-permute-done((bf16[1360,1024]{1,0:T(8,128)(2,1)}, bf16[1360,1024]{1,0:T(8,128)(2,1)}, u32[]{:S(2)}, u32[]{:S(2)}) %collective-permute-start.2) | collective-permute-done | bytes 2785312 | tf_op jit(solution)/shard_map/ppermute | solution.py:14
  365.6 7.7 fusion.97
  373.4 12.9 %convert_reduce_fusion.2 = (f32[1024]{0:T(1024)S(1)}, bf16[1360,1024]{1,0:T(8,128)(2,1)}, f32[1360,1024]{1,0:T(8,128)}, f32[1360,1024]{1,0:T(8,128)}, bf16[1360,1024]{1,0:T(8,128)(2,1)}, /*index=5*/f32[1360,1024]{1,0:T(8,128)}) fusion(f32[2,1024]{1,0:T(2,128)S(1)} %get-tuple-element.56, f32[1360]{0:T(1024)S(1)} %broadcast_multiply_fusion.2, ...), kind=kLoop, calls=%fused_computation.40 | loop fusion | flops 32029696 | bytes 41833728 | tf_op jit(solution)/shard_map/reduce_sum | solution.py:142
  399.6 16.4 %fusion.48 = bf16[2,680,8,64]{1,3,2,0:T(8,128)(2,1)} fusion(bf16[2,680,8,64]{1,3,2,0:T(8,128)(2,1)} %copy.66, f32[2,8,680,680]{2,3,1,0:T(8,128)} %get-tuple-element.64, f32[2,8,680]{2,1,0:T(8,128)S(1)} %log_add_fusion, pred[2,680,680]{1,2,0:T(8,128)(4,1)} %broadcast_compare_fusion), kind=kOutput, calls=%fused_computation.102 | convolution fusion | flops 969886720 | bytes 33347200 | tf_op jit(solution)/shard_map/ihst,ishe->ithe/dot_general | solution.py:155
  416.0 30.9 %multiply_reduce_fusion = (f32[2,8,680]{2,1,0:T(8,128)S(1)}, f32[2,8,680,680]{2,3,1,0:T(8,128)}) fusion(f32[2,8,680,680]{2,3,1,0:T(8,128)} %get-tuple-element.64, f32[2,8,680]{2,1,0:T(8,128)S(1)} %log_add_fusion, pred[2,680,680]{1,2,0:T(8,128)(4,1)} %broadcast_compare_fusion, bf16[2,680,8,64]{1,3,2,0:T(8,128)(2,1)} %copy.66, ...), kind=kOutput, calls=%fused_computation.3 | convolution fusion | flops 976577920 | bytes 62984320 | tf_op jit(solution)/shard_map/ishe,ithe->ihst/dot_general | solution.py:149
  446.9 28.4 %multiply_convert_fusion = bf16[2,8,680,680]{2,3,1,0:T(8,128)(2,1)} fusion(f32[2,8,680,680]{2,3,1,0:T(8,128)} %get-tuple-element.66, f32[2,8,680,680]{2,3,1,0:T(8,128)} %get-tuple-element.64, f32[2,8,680]{2,1,0:T(8,128)S(1)} %get-tuple-element.65, f32[2,8,680]{2,1,0:T(8,128)S(1)} %log_add_fusion, pred[2,680,680]{1,2,0:T(8,128)(4,1)} %broadcast_compare_fusion), kind=kLoop, calls=%fused_computation.2 | loop fusion | flops 36992000 | bytes 74995840 | tf_op jit(solution)/shard_map/convert_element_type | solution.py:152
  475.4 11.5 %fusion.95 = f32[2,8,64,680]{3,2,1,0:T(8,128)} fusion(bf16[2,8,680,680]{2,3,1,0:T(8,128)(2,1)} %multiply_convert_fusion, f32[2,680,1,8,64]{1,4,3,0,2:T(8,128)} %copy.88, f32[8]{0:T(128)S(1)} %copy-done.31, f32[2,680,8]{1,2,0:T(8,128)S(1)} %copy-done.13), kind=kOutput, calls=%fused_computation.186 | convolution fusion | flops 949084160 | bytes 20410912 | tf_op jit(solution)/shard_map/ihst,ishe->ithe/dot_general | solution.py:154
  486.9 10.5 %fusion.25 = (f32[8]{0:T(128)S(1)}, f32[2,8,64,680]{3,2,1,0:T(8,128)}) fusion(f32[2,680,1,8,64]{1,4,3,0,2:T(8,128)S(1)} %copy-done.5, f32[8]{0:T(128)S(1)} %copy-done.31, f32[2,680,8]{1,2,0:T(8,128)S(1)} %copy-done.13, bf16[2,8,680,680]{2,3,1,0:T(8,128)(2,1)} %multiply_convert_fusion, f32[2,680,1,8,64]{1,4,3,0,2:T(8,128)S(1)} %copy-done.7, ...), kind=kOutput, calls=%fused_computation.74 | convolution fusion | flops 951173120 | bytes 23239744 | tf_op jit(solution)/shard_map/ihst,ithe->ishe/dot_general | solution.py:153
  507.3 6.8 fusion.24
  534.5 8.2 bitcast_convert_fusion
  544.1 11.0 %convolution_convert_fusion.3 = bf16[1024,2048]{1,0:T(8,128)(2,1)} fusion(bf16[1360,1024]{1,0:T(8,128)(2,1)S(1)} %copy-done.18, bf16[1360,2048]{1,0:T(8,128)(2,1)} %get-tuple-element.32), kind=kOutput, calls=%fused_computation.65 | convolution fusion | flops 5706350592 | bytes 12550144 | tf_op jit(solution)/shard_map/rd,rf->df/dot_general | solution.py:133
  556.9 9.4 fusion.35
  566.4 34.9 %collective-permute-done.3 = bf16[1360,1024]{1,0:T(8,128)(2,1)} collective-permute-done((bf16[1360,1024]{1,0:T(8,128)(2,1)}, bf16[1360,1024]{1,0:T(8,128)(2,1)}, u32[]{:S(2)}, u32[]{:S(2)}) %collective-permute-start.3) | collective-permute-done | bytes 2785312 | tf_op jit(solution)/shard_map/ppermute | solution.py:14
  604.6 6.5 fusion.96
  616.7 9.6 multiply_reduce_fusion.1
  685.2 36.2 %all-reduce.5.cloned.1.call-done = f32[82048]{0:T(1024)} async-done(((f32[82048]{0:T(1024)}), f32[82048]{0:T(1024)}) %all-reduce.5.cloned.1.call-update) | async-done | bytes 328208
  727.5 6.8 fusion.66
  737.5 222.4 %all-reduce.7.cloned.1.call-done = (bf16[1024,3,512]{2,0,1:T(8,128)(2,1)}, bf16[512,1024]{1,0:T(8,128)(2,1)}, bf16[1024,2048]{1,0:T(8,128)(2,1)}, bf16[2048,1024]{1,0:T(8,128)(2,1)}) async-done(((bf16[1024,3,512]{2,0,1:T(8,128)(2,1)}, bf16[512,1024]{1,0:T(8,128)(2,1)}, bf16[1024,2048]{1,0:T(8,128)(2,1)}, bf16[2048,1024]{1,0:T(8,128)(2,1)}), (bf16[1024,3,512]{2,0,1:T(8,128)(2,1)}, ...) | async-done | bytes 12582928 | tf_op jit(solution)/shard_map/psum | solution.py:226
  (261 shorter events, 218.8 us)
Async XLA Ops:
  8.0 25.7 %copy-start = (bf16[1024,3,512]{2,0,1:T(8,128)(2,1)S(1)}, bf16[1024,3,512]{2,0,1:T(8,128)(2,1)}, u32[]{:S(2)}) copy-start(bf16[1024,3,512]{2,0,1:T(8,128)(2,1)} %param.24) | copy-start | bytes 9437188
  8.1 713.4 %all-reduce.5.cloned.1.call-start = ((), (), s32[]{:S(2)}) async-start(), calls=%async_computation.2 | async-start | bytes 663552
  12.0 141.3 %copy-start.25 = (f32[1360]{0:T(1024)}, f32[1360]{0:T(1024)S(1)}, u32[]{:S(2)}) copy-start(f32[1360]{0:T(1024)S(1)} %broadcast_multiply_fusion.5) | copy-start | bytes 16324
  14.7 139.3 %copy-start.28 = (f32[1360]{0:T(1024)}, f32[1360]{0:T(1024)S(1)}, u32[]{:S(2)}) copy-start(f32[1360]{0:T(1024)S(1)} %add_rsqrt_fusion.3) | copy-start | bytes 16324
  151.3 60.4 %collective-permute-start = (bf16[1360,1024]{1,0:T(8,128)(2,1)}, bf16[1360,1024]{1,0:T(8,128)(2,1)}, u32[]{:S(2)}, u32[]{:S(2)}) collective-permute-start(bf16[1360,1024]{1,0:T(8,128)(2,1)} %convolution_convert_fusion.4), channel_id=1, source_target_pairs={{0,1},{1,0},{2,3},{3,2},{4,5},{5,4},{6,7},{7,6},{8,9},{9,8},{10,11... | collective-permute-start | bytes 8355848 | tf_op jit(solution)/shard_map/ppermute | solution.py:14
  243.2 130.2 %collective-permute-start.1 = (bf16[1360,1024]{1,0:T(8,128)(2,1)}, bf16[1360,1024]{1,0:T(8,128)(2,1)}, u32[]{:S(2)}, u32[]{:S(2)}) collective-permute-start(bf16[1360,1024]{1,0:T(8,128)(2,1)} %convolution_convert_fusion.1), channel_id=1, source_target_pairs={{0,1},{1,0},{2,3},{3,2},{4,5},{5,4},{6,7},{7,6},{8,9},{9,8},{10,11... | collective-permute-start | bytes 8355848 | tf_op jit(solution)/shard_map/ppermute | solution.py:14
  271.7 90.7 %collective-permute-start.2 = (bf16[1360,1024]{1,0:T(8,128)(2,1)}, bf16[1360,1024]{1,0:T(8,128)(2,1)}, u32[]{:S(2)}, u32[]{:S(2)}) collective-permute-start(bf16[1360,1024]{1,0:T(8,128)(2,1)} %convolution_convert_fusion), channel_id=1, source_target_pairs={{0,1},{1,0},{2,3},{3,2},{4,5},{5,4},{6,7},{7,6},{8,9},{9,8},{10,11... | collective-permute-start | bytes 8355848 | tf_op jit(solution)/shard_map/ppermute | solution.py:14
  446.9 28.4 %copy-start.13 = (f32[2,680,8]{1,2,0:T(8,128)S(1)}, f32[2,680,8]{1,2,0:T(8,128)}, u32[]{:S(2)}) copy-start(f32[2,680,8]{1,2,0:T(8,128)} %copy-done.12) | copy-start | bytes 130564
  446.9 28.5 %copy-start.31 = (f32[8]{0:T(128)S(1)}, f32[8]{0:T(128)}, u32[]{:S(2)}) copy-start(f32[8]{0:T(128)} %copy-done.30) | copy-start | bytes 100
  542.6 58.7 %collective-permute-start.3 = (bf16[1360,1024]{1,0:T(8,128)(2,1)}, bf16[1360,1024]{1,0:T(8,128)(2,1)}, u32[]{:S(2)}, u32[]{:S(2)}) collective-permute-start(bf16[1360,1024]{1,0:T(8,128)(2,1)} %bitcast_convert_fusion), channel_id=1, source_target_pairs={{0,1},{1,0},{2,3},{3,2},{4,5},{5,4},{6,7},{7,6},{8,9},{9,8},{10,11... | collective-permute-start | bytes 8355848 | tf_op jit(solution)/shard_map/ppermute | solution.py:14
  556.9 44.4 %copy-start.33 = (f32[2,1024]{1,0:T(2,128)S(1)}, f32[2,1024]{1,0:T(2,128)}, u32[]{:S(2)}) copy-start(f32[2,1024]{1,0:T(2,128)} %copy-done.32) | copy-start | bytes 24580
  566.3 38.2 %copy-start.4 = (bf16[1360,1024]{1,0:T(8,128)(2,1)S(1)}, bf16[1360,1024]{1,0:T(8,128)(2,1)}, u32[]{:S(2)}) copy-start(bf16[1360,1024]{1,0:T(8,128)(2,1)} %param.17) | copy-start | bytes 8355844
  566.3 38.2 %copy-start.26 = (f32[1360]{0:T(1024)S(1)}, f32[1360]{0:T(1024)}, u32[]{:S(2)}) copy-start(f32[1360]{0:T(1024)} %copy-done.25) | copy-start | bytes 16324
  566.4 38.2 %copy-start.29 = (f32[1360]{0:T(1024)S(1)}, f32[1360]{0:T(1024)}, u32[]{:S(2)}) copy-start(f32[1360]{0:T(1024)} %copy-done.28) | copy-start | bytes 16324
  626.4 7.2 collective-permute-start.4
  626.4 7.2 collective-permute-start.5
  633.5 100.8 %reduce-scatter.2.cloned.1.call-start = ((), (), s32[]{:S(2)}) async-start(), calls=%async_computation.1 | async-start | bytes 196608 | tf_op jit(solution)/shard_map/reduce_scatter | solution.py:217
  633.6 5.9 collective-permute-start.6
  633.7 5.8 collective-permute-start.7
  639.5 5.8 collective-permute-start.8
  639.5 5.8 collective-permute-start.9
  645.3 5.8 collective-permute-start.10
  645.3 5.9 collective-permute-start.11
  651.1 5.8 collective-permute-start.12
  651.2 5.8 collective-permute-start.13
  657.0 5.8 collective-permute-start.14
  657.0 5.9 collective-permute-start.15
  662.8 5.8 collective-permute-start.16
  662.9 5.8 collective-permute-start.17
  668.6 5.8 collective-permute-start.18
  679.9 280.0 %all-reduce.7.cloned.1.call-start = ((), (), s32[]{:S(2)}) async-start(), calls=%async_computation.3 | async-start | bytes 25165824 | tf_op jit(solution)/shard_map/psum | solution.py:226
  685.2 42.3 %copy-start.24 = (bf16[32,1024]{1,0:T(8,128)(2,1)S(1)}, bf16[32,1024]{1,0:T(8,128)(2,1)}, u32[]{:S(2)}) copy-start(bf16[32,1024]{1,0:T(8,128)(2,1)} %copy-done.23) | copy-start | bytes 196612
  (46 other events, 427.8 us)
Sparse Core Ops, SparseCore 0:
  633.6 87.7 all-reduce.4
  726.6 233.2 all-reduce.6
Sparse Core Ops, SparseCore 1:
  680.0 7.2 reduce-scatter.1
